TPU v7x, 32 devices: a whole 2x2x4 slice. The times are simulated.
32 devices in a mesh: rp: 2 (over x), pb: 16 (over z, y, core).
Axes of the slice: x: 2, y: 2, z: 4, core: 2. Of those that a mesh axis runs over, the one named last changes fastest.
Arguments:
- wannier_g: bfloat16 [2, 1024, 32, 1152], P(None, 'rp', 'pb'), may hold values from -0.19921875 to 0.19921875
- rp_coords: int32 [3, 1024], replicated, may hold values from -8 to 8
- q_coords: int32 [3, 64], P(None, ('rp', 'pb')), may hold values from 0 to 15
- k_index: int32 [1], replicated, may hold values from 0 to 7
- k_vectors: bfloat16 [8, 2, 32, 32], replicated, may hold values from -0.75 to 0.75
- kq_vectors: bfloat16 [64, 2, 32, 32], P(('rp', 'pb')), may hold values from -0.75 to 0.75
- modes: bfloat16 [64, 2, 36, 36], P(('rp', 'pb')), may hold values from -0.75 to 0.75
Outputs:
- rotated: float32 [64, 2, 32, 1152], P(('rp', 'pb'))
All inputs are finite; a program needn't handle non-finite values.
Results may differ from a plain program's by a relative error of at most 0.0054.
Values may be sent and summed in bfloat16 or wider, within the bound.
A program may use at most 64 MiB of HBM per device.

v0:
```python
import math
import jax
import jax.numpy as jnp
from jax import lax
from jax.sharding import PartitionSpec as P

NK = 16


def phases(q_rows, r_coords):
    turns = jnp.mod(jnp.sum(q_rows[:, :, None] * r_coords[:, None, :], axis=0), NK)
    angle = turns.astype(jnp.float32) * (2.0 * math.pi / NK)
    cosine = jnp.cos(angle).astype(jnp.bfloat16)
    sine = jnp.sin(angle).astype(jnp.bfloat16)
    return (jnp.concatenate([cosine, -sine], axis=1), jnp.concatenate([sine, cosine], axis=1))


def rotate(fourier, mode_vecs, unit, kq_vecs):
    count = fourier.shape[0]
    bands = kq_vecs.shape[2]
    branches = mode_vecs.shape[2]
    field = fourier.reshape(count, 2, bands, bands, branches)
    e_real, e_imag = (mode_vecs[:, 0], mode_vecs[:, 1])
    e_block = jnp.stack([jnp.stack([e_real, e_imag], 2), jnp.stack([-e_imag, e_real], 2)], 1)
    by_mode = jnp.einsum(
        "qcmnv,qcvdu->qdmnu", field, e_block, preferred_element_type=jnp.float32
    ).astype(jnp.bfloat16)
    u_real, u_imag = (unit[0], unit[1])
    u_block = jnp.stack([jnp.stack([u_real, u_imag], 1), jnp.stack([-u_imag, u_real], 1)], 0)
    by_band = jnp.einsum(
        "qcmnu,cndj->qdmju", by_mode, u_block, preferred_element_type=jnp.float32
    ).astype(jnp.bfloat16)
    v_real, v_imag = (kq_vecs[:, 0], kq_vecs[:, 1])
    v_block = jnp.stack([jnp.stack([v_real, -v_imag], 2), jnp.stack([v_imag, v_real], 2)], 1)
    result = jnp.einsum("qcmju,qcmdi->qdiju", by_band, v_block, preferred_element_type=jnp.float32)
    return result.reshape(count, 2, bands, bands * branches)


def body(wannier_g, rp_coords, q_coords, k_index, k_vectors, kq_vectors, modes):
    q_all = lax.all_gather(q_coords, ("rp", "pb"), axis=1, tiled=True)
    total = q_all.shape[1]
    groups = lax.axis_size("rp")
    block = total // groups
    local = wannier_g.shape[1]
    own_coords = lax.dynamic_slice_in_dim(rp_coords, lax.axis_index("rp") * local, local, 1)
    right = wannier_g.reshape(2 * local, -1)
    left_real, left_imag = phases(q_all, own_coords)
    f_real = jnp.dot(left_real, right, preferred_element_type=jnp.float32)
    f_imag = jnp.dot(left_imag, right, preferred_element_type=jnp.float32)
    summed = lax.psum_scatter(jnp.stack([f_real, f_imag], 1), "rp", scatter_dimension=0, tiled=True)
    fourier = summed.astype(jnp.bfloat16).reshape(block, 2, wannier_g.shape[2], wannier_g.shape[3])
    owned = lax.all_to_all(fourier, "pb", split_axis=0, concat_axis=2, tiled=True)
    select = (jnp.arange(k_vectors.shape[0]) == k_index[0]).astype(jnp.bfloat16)
    unit = jnp.einsum("k,kcnj->cnj", select, k_vectors, preferred_element_type=jnp.float32).astype(
        jnp.bfloat16
    )
    return rotate(owned, modes, unit, kq_vectors)


def solution(mesh):
    return jax.shard_map(
        body,
        mesh=mesh,
        in_specs=(
            P(None, "rp", "pb", None),
            P(),
            P(None, ("rp", "pb")),
            P(),
            P(),
            P(("rp", "pb"), None, None, None),
            P(("rp", "pb"), None, None, None),
        ),
        out_specs=P(("rp", "pb"), None, None, None),
        check_vma=False,
    )
```

profile of v0, /device:TPU:0, one launch (start us, length us, event | category | flops | bytes accessed | tf_op | source)
XLA Modules:
  0.0 110.1 jit_solution(14693091623832037747)
XLA Ops:
  6.5 0.0 copy-start
  6.5 0.0 reduce-scatter.2.cloned.1.call-start
  6.5 43.7 %all-gather = s32[32,2,3]{2,1,0:T(2,128)S(1)} all-gather(s32[1,2,3]{2,1,0:T(2,128)} %bitcast.115), channel_id=1, replica_groups=mesh['rp'=2,'pb'=16] {'rp','pb'}, dimensions={0}, use_global_device_ids=true | all-gather | bytes 792 | tf_op jit(solution)/shard_map/all_gather | solution.py:40
  50.2 0.1 copy.76
  50.3 0.7 constant_dynamic-slice_fusion
  51.0 0.1 multiply_reduce_fusion
  51.1 0.5 fusion.32
  51.6 0.5 cosine_convert_fusion
  52.1 3.2 %copy.104 = bf16[128,8,2,1152]{3,1,2,0:T(8,128)(2,1)S(1)} copy(bf16[128,8,2,1152]{3,2,1,0:T(2,128)(2,1)} %bitcast.107) | data formatting | bytes 9437184
  55.3 0.9 convolution_bitcast_fusion.1
  56.2 0.9 convolution_bitcast_fusion
  57.1 0.0 copy-start.1
  57.2 0.0 copy-start.2
  57.2 1.1 pad_maximum_fusion
  58.3 0.0 reduce-scatter.2.cloned.1.call-update
  58.3 0.0 copy-done.1
  58.3 0.1 fusion.33
  59.0 0.0 copy-done
  59.1 0.2 fusion.15
  59.3 0.1 copy.86
  59.3 0.0 copy-done.2
  59.4 0.1 copy.102
  59.4 0.1 copy.101
  59.6 17.1 %reduce-scatter.2.cloned.1.call-done = f32[32,2,2304]{2,0,1:T(8,128)} async-done(((f32[64,2,2304]{2,0,1:T(8,128)}), f32[32,2,2304]{2,0,1:T(8,128)}) %reduce-scatter.2.cloned.1.call-update) | async-done | bytes 589840 | tf_op jit(solution)/shard_map/reduce_scatter | solution.py:50
  76.7 1.1 convert_element_type.32
  77.8 0.1 reshape.46
  77.8 0.9 copy.77
  78.7 5.6 %all-to-all-start = ((bf16[32,2,2,1152]{3,2,1,0:T(2,128)(2,1)}), bf16[32,2,2,1152]{3,2,1,0:T(2,128)(2,1)S(1)}, u32[]{:S(2)}, u32[]{:S(2)}) async-start(bf16[32,2,2,1152]{3,2,1,0:T(2,128)(2,1)} %copy.77), calls=%async_computation.1 | async-start | bytes 589824 | tf_op jit(solution)/shard_map/all_to_all | solution.py:52
  84.4 0.1 maximum_bitcast_fusion.3
  84.5 0.1 maximum_bitcast_fusion
  84.7 10.2 %all-to-all-done = bf16[32,2,2,1152]{3,2,1,0:T(2,128)(2,1)S(1)} async-done(((bf16[32,2,2,1152]{3,2,1,0:T(2,128)(2,1)}), bf16[32,2,2,1152]{3,2,1,0:T(2,128)(2,1)S(1)}, u32[]{:S(2)}, u32[]{:S(2)}) %all-to-all-start) | async-done | bytes 294944 | tf_op jit(solution)/shard_map/all_to_all | solution.py:52
  94.9 0.2 copy.97
  95.1 3.0 %reshape.54 = bf16[2,2,32,32,36,1]{4,3,1,2,0,5:T(8,128)(2,1)S(1)} reshape(bf16[2,2,16,2,1152]{4,1,3,2,0:T(2,128)(2,1)S(1)} %copy.97) | data formatting | bytes 589824 | tf_op jit(solution)/shard_map/reshape | solution.py:22
  98.1 0.5 fusion
  98.6 0.5 fusion.1
  99.1 0.5 convolution_bitcast_fusion.2
  99.6 1.2 %copy.83 = f32[2,2,32,32,36]{4,3,2,1,0:T(8,128)S(1)} copy(f32[2,2,32,32,36]{4,2,3,1,0:T(8,128)S(1)} %convolution_bitcast_fusion.2) | data formatting | bytes 1179648 | tf_op jit(solution)/shard_map/qcmju,qcmdi->qdiju/dot_general | solution.py:35
  100.8 2.4 %reshape.48 = f32[2,2,32,1152]{3,2,1,0:T(8,128)} reshape(f32[2,2,32,32,36]{4,3,2,1,0:T(8,128)S(1)} %copy.83) | data formatting | bytes 1179648 | tf_op jit(solution)/shard_map/reshape | solution.py:36
  (8 shorter events, 0.1 us)
Async XLA Ops:
  6.5 52.5 %copy-start = (bf16[8,2,32,32]{3,2,1,0:T(8,128)(2,1)S(1)}, bf16[8,2,32,32]{3,2,1,0:T(8,128)(2,1)}, u32[]{:S(2)}) copy-start(bf16[8,2,32,32]{3,2,1,0:T(8,128)(2,1)} %param.11) | copy-start | bytes 98308
  6.5 70.1 %reduce-scatter.2.cloned.1.call-start = ((), (), s32[]{:S(2)}) async-start(), calls=%async_computation.2 | async-start | bytes 1769472 | tf_op jit(solution)/shard_map/reduce_scatter | solution.py:50
  57.1 1.1 %copy-start.1 = (bf16[2,2,36,36]{3,1,2,0:T(2,128)(2,1)S(1)}, bf16[2,2,36,36]{3,1,2,0:T(2,128)(2,1)}, u32[]{:S(2)}) copy-start(bf16[2,2,36,36]{3,1,2,0:T(2,128)(2,1)} %param.13) | copy-start | bytes 31108
  57.2 2.2 %copy-start.2 = (bf16[2,2,32,32]{3,2,1,0:T(8,128)(2,1)S(1)}, bf16[2,2,32,32]{3,2,1,0:T(8,128)(2,1)}, u32[]{:S(2)}) copy-start(bf16[2,2,32,32]{3,2,1,0:T(8,128)(2,1)} %param.12) | copy-start | bytes 24580
  78.7 16.2 %all-to-all-start = ((bf16[32,2,2,1152]{3,2,1,0:T(2,128)(2,1)}), bf16[32,2,2,1152]{3,2,1,0:T(2,128)(2,1)S(1)}, u32[]{:S(2)}, u32[]{:S(2)}) async-start(bf16[32,2,2,1152]{3,2,1,0:T(2,128)(2,1)} %copy.77), calls=%async_computation.1 | async-start | bytes 589824 | tf_op jit(solution)/shard_map/all_to_all | solution.py:52
Sparse Core Ops, SparseCore 0:
  58.4 18.1 reduce-scatter.1
where the time goes:
time: 110 us
  blocking collectives  43.7 us (40%)
  waiting for transfers between devices  27.3 us (25%)
  between operations  14.3 us (13%)
  local copies, waits for them, and re-layouts  12.2 us (11%)
  starting transfers between devices  5.61 us (5%)
  other arithmetic  3.58 us (3%)
  matrix products  3.51 us (3%)
    all_gather x1, blocking collectives, body(): q_all = lax.all_gather(q_coords, ('rp', 'pb'), axis=1, tiled=True)  43.7 us
    reduce_scatter x1, waiting for transfers between devices, body(): lax.psum_scatter(jnp.stack([f_real, f_imag], 1), 'rp', scatter_dimension=...  17.1 us
    all_to_all x1, waiting for transfers between devices, body(): lax.all_to_all(fourier, 'pb', split_axis=0, concat_axis=2, tiled=True)  10.2 us
    all_to_all x1, starting transfers between devices, body(): lax.all_to_all(fourier, 'pb', split_axis=0, concat_axis=2, tiled=True)  5.61 us
    unnamed x11, local copies, waits for them, and re-layouts  3.46 us
    reshape x2, local copies, waits for them, and re-layouts, rotate(): field = fourier.reshape(count, 2, bands, bands, branches)  3.2 us
    reshape x1, local copies, waits for them, and re-layouts, rotate(): return result.reshape(count, 2, bands, bands * branches)  2.44 us
  transfers between devices with their start and end apart: 2, of which 2 were waited for; matrix products, arithmetic and copies ran while one was open for 1% of the time, Pallas kernels for 0%

commit v1 on v0

--- a/solution.py
+++ b/solution.py
@@ -37,7 +37,8 @@
 
 
 def body(wannier_g, rp_coords, q_coords, k_index, k_vectors, kq_vectors, modes):
-    q_all = lax.all_gather(q_coords, ("rp", "pb"), axis=1, tiled=True)
+    shards = lax.all_gather(q_coords, ("rp", "pb"))
+    q_all = jnp.concatenate(shards, axis=1)
     total = q_all.shape[1]
     groups = lax.axis_size("rp")
     block = total // groups

time: 110 us -> 110 us (level)
    unnamed x11 -> x10, local copies, waits for them, and re-layouts: 3.46 us -> 3.39 us
where the time goes in v1:
time: 110 us
  blocking collectives  43.7 us (40%)
  waiting for transfers between devices  27.3 us (25%)
  between operations  14.3 us (13%)
  local copies, waits for them, and re-layouts  12.2 us (11%)
  starting transfers between devices  5.61 us (5%)
  other arithmetic  3.58 us (3%)
  matrix products  3.51 us (3%)
    all_gather x1, blocking collectives, body(): shards = lax.all_gather(q_coords, ('rp', 'pb'))  43.7 us
    reduce_scatter x1, waiting for transfers between devices, body(): lax.psum_scatter(jnp.stack([f_real, f_imag], 1), 'rp', scatter_dimension=...  17.1 us
    all_to_all x1, waiting for transfers between devices, body(): lax.all_to_all(fourier, 'pb', split_axis=0, concat_axis=2, tiled=True)  10.2 us
    all_to_all x1, starting transfers between devices, body(): lax.all_to_all(fourier, 'pb', split_axis=0, concat_axis=2, tiled=True)  5.61 us
    unnamed x10, local copies, waits for them, and re-layouts  3.39 us
    reshape x2, local copies, waits for them, and re-layouts, rotate(): field = fourier.reshape(count, 2, bands, bands, branches)  3.2 us
    reshape x1, local copies, waits for them, and re-layouts, rotate(): return result.reshape(count, 2, bands, bands * branches)  2.44 us
  transfers between devices with their start and end apart: 2, of which 2 were waited for; matrix products, arithmetic and copies ran while one was open for 1% of the time, Pallas kernels for 0%

profile of v1, /device:TPU:0, one launch (start us, length us, event | category | flops | bytes accessed | tf_op | source)
XLA Modules:
  0.0 110.1 jit_solution(14693091623832037747)
XLA Ops:
  6.5 0.0 copy-start
  6.5 0.0 reduce-scatter.2.cloned.1.call-start
  6.5 43.7 %all-gather.1 = s32[32,3,2]{1,2,0:T(2,128)S(1)} all-gather(s32[1,3,2]{1,2,0:T(2,128)} %bitcast.113), channel_id=2, replica_groups=mesh['rp'=2,'pb'=16] {'rp','pb'}, dimensions={0}, use_global_device_ids=true | all-gather | bytes 792 | tf_op jit(solution)/shard_map/all_gather | solution.py:40
  50.2 0.1 copy.76
  50.3 0.7 constant_dynamic-slice_fusion
  51.0 0.1 multiply_reduce_fusion
  51.1 0.5 fusion.32
  51.6 0.5 cosine_convert_fusion
  52.1 3.2 %copy.104 = bf16[128,8,2,1152]{3,1,2,0:T(8,128)(2,1)S(1)} copy(bf16[128,8,2,1152]{3,2,1,0:T(2,128)(2,1)} %bitcast.105) | data formatting | bytes 9437184
  55.3 0.9 convolution_bitcast_fusion.1
  56.2 0.9 convolution_bitcast_fusion
  57.1 0.0 copy-start.1
  57.2 0.0 copy-start.2
  57.2 1.1 pad_maximum_fusion
  58.3 0.0 reduce-scatter.2.cloned.1.call-update
  58.3 0.0 copy-done.1
  58.3 0.1 fusion.33
  59.0 0.0 copy-done
  59.1 0.2 fusion.15
  59.3 0.1 copy.86
  59.3 0.0 copy-done.2
  59.4 0.1 copy.102
  59.4 0.1 copy.101
  59.6 17.1 %reduce-scatter.2.cloned.1.call-done = f32[32,2,2304]{2,0,1:T(8,128)} async-done(((f32[64,2,2304]{2,0,1:T(8,128)}), f32[32,2,2304]{2,0,1:T(8,128)}) %reduce-scatter.2.cloned.1.call-update) | async-done | bytes 589840 | tf_op jit(solution)/shard_map/reduce_scatter | solution.py:51
  76.7 1.1 convert_element_type.32
  77.8 0.1 reshape.50
  77.8 0.9 copy.77
  78.7 5.6 %all-to-all-start = ((bf16[32,2,2,1152]{3,2,1,0:T(2,128)(2,1)}), bf16[32,2,2,1152]{3,2,1,0:T(2,128)(2,1)S(1)}, u32[]{:S(2)}, u32[]{:S(2)}) async-start(bf16[32,2,2,1152]{3,2,1,0:T(2,128)(2,1)} %copy.77), calls=%async_computation.1 | async-start | bytes 589824 | tf_op jit(solution)/shard_map/all_to_all | solution.py:53
  84.4 0.1 maximum_bitcast_fusion.3
  84.5 0.1 maximum_bitcast_fusion
  84.7 10.2 %all-to-all-done = bf16[32,2,2,1152]{3,2,1,0:T(2,128)(2,1)S(1)} async-done(((bf16[32,2,2,1152]{3,2,1,0:T(2,128)(2,1)}), bf16[32,2,2,1152]{3,2,1,0:T(2,128)(2,1)S(1)}, u32[]{:S(2)}, u32[]{:S(2)}) %all-to-all-start) | async-done | bytes 294944 | tf_op jit(solution)/shard_map/all_to_all | solution.py:53
  94.9 0.2 copy.97
  95.1 3.0 %reshape.60 = bf16[2,2,32,32,36,1]{4,3,1,2,0,5:T(8,128)(2,1)S(1)} reshape(bf16[2,2,16,2,1152]{4,1,3,2,0:T(2,128)(2,1)S(1)} %copy.97) | data formatting | bytes 589824 | tf_op jit(solution)/shard_map/reshape | solution.py:22
  98.1 0.5 fusion
  98.6 0.5 fusion.1
  99.1 0.5 convolution_bitcast_fusion.2
  99.6 1.2 %copy.83 = f32[2,2,32,32,36]{4,3,2,1,0:T(8,128)S(1)} copy(f32[2,2,32,32,36]{4,2,3,1,0:T(8,128)S(1)} %convolution_bitcast_fusion.2) | data formatting | bytes 1179648 | tf_op jit(solution)/shard_map/qcmju,qcmdi->qdiju/dot_general | solution.py:35
  100.8 2.4 %reshape.52 = f32[2,2,32,1152]{3,2,1,0:T(8,128)} reshape(f32[2,2,32,32,36]{4,3,2,1,0:T(8,128)S(1)} %copy.83) | data formatting | bytes 1179648 | tf_op jit(solution)/shard_map/reshape | solution.py:36
  (8 shorter events, 0.1 us)
Async XLA Ops:
  6.5 52.5 %copy-start = (bf16[8,2,32,32]{3,2,1,0:T(8,128)(2,1)S(1)}, bf16[8,2,32,32]{3,2,1,0:T(8,128)(2,1)}, u32[]{:S(2)}) copy-start(bf16[8,2,32,32]{3,2,1,0:T(8,128)(2,1)} %param.11) | copy-start | bytes 98308
  6.5 70.1 %reduce-scatter.2.cloned.1.call-start = ((), (), s32[]{:S(2)}) async-start(), calls=%async_computation.2 | async-start | bytes 1769472 | tf_op jit(solution)/shard_map/reduce_scatter | solution.py:51
  57.1 1.1 %copy-start.1 = (bf16[2,2,36,36]{3,1,2,0:T(2,128)(2,1)S(1)}, bf16[2,2,36,36]{3,1,2,0:T(2,128)(2,1)}, u32[]{:S(2)}) copy-start(bf16[2,2,36,36]{3,1,2,0:T(2,128)(2,1)} %param.13) | copy-start | bytes 31108
  57.2 2.2 %copy-start.2 = (bf16[2,2,32,32]{3,2,1,0:T(8,128)(2,1)S(1)}, bf16[2,2,32,32]{3,2,1,0:T(8,128)(2,1)}, u32[]{:S(2)}) copy-start(bf16[2,2,32,32]{3,2,1,0:T(8,128)(2,1)} %param.12) | copy-start | bytes 24580
  78.7 16.2 %all-to-all-start = ((bf16[32,2,2,1152]{3,2,1,0:T(2,128)(2,1)}), bf16[32,2,2,1152]{3,2,1,0:T(2,128)(2,1)S(1)}, u32[]{:S(2)}, u32[]{:S(2)}) async-start(bf16[32,2,2,1152]{3,2,1,0:T(2,128)(2,1)} %copy.77), calls=%async_computation.1 | async-start | bytes 589824 | tf_op jit(solution)/shard_map/all_to_all | solution.py:53
Sparse Core Ops, SparseCore 0:
  58.4 18.1 reduce-scatter.1
